TPU v7x, 32 devices: a whole 2x2x4 slice. The times are simulated.
32 devices in a mesh: blk: 4 (over y, x), grp: 8 (over z, core).
Axes of the slice: x: 2, y: 2, z: 4, core: 2. Of those that a mesh axis runs over, the one named last changes fastest.
Arguments:
- queries: bfloat16 [32, 32, 128], P('blk', 'grp'), may hold values from -3 to 3
- token_counts: int32 [32], P('blk'), may hold values from 8 to 32
- pages: bfloat16 [32, 1024, 128], P(('blk', 'grp')), may hold values from -6 to 6
- patch_counts: int32 [32], P(('blk', 'grp')), may hold values from 512 to 1024
- labels: int32 [32, 32], P(None, ('blk', 'grp')), may hold values 0 or 1
Outputs:
- query_grad: float32 [32, 32, 128], P('blk', 'grp')
- page_grad: float32 [32, 1024, 128], P(('blk', 'grp'))
- page_loss: float32 [32], P(('blk', 'grp'))
All inputs are finite; a program needn't handle non-finite values. No bound on the sum of `labels` on one device may be relied on, other than what follows from the above.
Results may differ from a plain program's by a relative error of at most 0.018.
Values may be sent and summed in bfloat16 or wider, within the bound.
A program may use at most 64 MiB of HBM per device.

v0:
```python
import jax
import jax.numpy as jnp
from jax import lax
from jax.sharding import PartitionSpec as P

align_sharpness = 4.0
logit_scale = 2.0
logit_bias = -5.0


def align(query_rows, counts, page_rows, patch_count, label_column):
    query_number = counts.shape[0]
    token_slots = query_rows.shape[0] // query_number
    scores = jnp.dot(query_rows, page_rows.T, preferred_element_type=jnp.float32)
    patch_mask = jnp.arange(page_rows.shape[0]) < patch_count
    logits = jnp.where(patch_mask[None, :], align_sharpness * scores, -jnp.inf)
    row_max = jnp.max(logits, axis=1, keepdims=True)
    exponent = jnp.exp(logits - row_max)
    weights = exponent / jnp.sum(exponent, axis=1, keepdims=True)
    token_score = jnp.sum(weights * scores, axis=1)
    token_mask = jnp.arange(token_slots)[None, :] < counts[:, None]
    count_float = counts.astype(jnp.float32)
    pair_score = (
        jnp.sum(
            jnp.where(token_mask, token_score.reshape(query_number, token_slots), jnp.float32(0.0)),
            axis=1,
        )
        / count_float
    )
    label_sign = 2.0 * label_column.astype(jnp.float32) - 1.0
    pair_logit = logit_scale * pair_score + logit_bias
    loss_sum = jnp.sum(jax.nn.softplus(-label_sign * pair_logit))
    score_grad = -label_sign * logit_scale * jax.nn.sigmoid(-label_sign * pair_logit)
    token_grad = jnp.where(
        token_mask, (score_grad / count_float)[:, None], jnp.float32(0.0)
    ).reshape(-1)
    scores_grad = (
        token_grad[:, None] * weights * (1.0 + align_sharpness * (scores - token_score[:, None]))
    ).astype(jnp.bfloat16)
    query_term = jnp.dot(scores_grad, page_rows, preferred_element_type=jnp.float32)
    page_term = jnp.dot(scores_grad.T, query_rows, preferred_element_type=jnp.float32)
    return (query_term, page_term, loss_sum)


def local(queries, token_counts, pages, patch_counts, labels):
    page_rows = pages[0]
    patch_count = patch_counts[0]
    label_column = labels[:, 0]
    feature_width = page_rows.shape[1]
    blocks = lax.axis_size("blk")
    groups = lax.axis_size("grp")
    block_queries = token_counts.shape[0]
    gathered = lax.all_gather(queries, "grp", axis=1, tiled=True)
    query_tokens = gathered.shape[1]
    total_queries = block_queries * blocks
    empty_page = jnp.zeros(page_rows.shape, jnp.float32)

    def block_terms(held_queries, held_counts, source):
        labels_here = lax.dynamic_slice_in_dim(label_column, source * block_queries, block_queries)
        return align(
            held_queries.reshape(-1, feature_width),
            held_counts,
            page_rows,
            patch_count,
            labels_here,
        )

    slice_tokens = query_tokens // groups
    buffer = jnp.zeros((blocks * groups * block_queries, slice_tokens, feature_width), jnp.float32)
    piece_queries = lax.all_gather(gathered, "blk", axis=0, tiled=True)
    piece_counts = lax.all_gather(token_counts, "blk", axis=0, tiled=True)
    count_blocks = piece_queries.shape[0] // block_queries

    def one_block(inner_index, state_in):
        page_grad, loss_sum, collected = state_in
        held_queries = lax.dynamic_slice_in_dim(
            piece_queries, inner_index * block_queries, block_queries
        )
        held_counts = lax.dynamic_slice_in_dim(
            piece_counts, inner_index * block_queries, block_queries
        )
        query_term, page_term, loss_term = block_terms(held_queries, held_counts, inner_index)
        arranged = query_term.reshape(block_queries, groups, slice_tokens, feature_width)
        arranged = arranged.transpose(1, 0, 2, 3).reshape(
            groups * block_queries, slice_tokens, feature_width
        )
        collected = lax.dynamic_update_slice_in_dim(
            collected, arranged, inner_index * groups * block_queries, 0
        )
        return (page_grad + page_term, loss_sum + loss_term, collected)

    page_grad, loss_sum, buffer = lax.fori_loop(
        0, count_blocks, one_block, (empty_page, jnp.float32(0.0), buffer)
    )
    query_grad = lax.psum_scatter(buffer, ("blk", "grp"), scatter_dimension=0, tiled=True)
    page_loss = (loss_sum / jnp.float32(total_queries)).reshape(1)
    return (query_grad, page_grad[None], page_loss)


def solution(mesh):
    in_specs = (
        P("blk", "grp", None),
        P("blk"),
        P(("blk", "grp"), None, None),
        P(("blk", "grp")),
        P(None, ("blk", "grp")),
    )
    out_specs = (P("blk", "grp", None), P(("blk", "grp"), None, None), P(("blk", "grp")))
    return jax.shard_map(local, mesh=mesh, in_specs=in_specs, out_specs=out_specs, check_vma=False)
```

profile of v0, /device:TPU:0, one launch (start us, length us, event | category | flops | bytes accessed | tf_op | source)
XLA Modules:
  0.0 203.5 jit_solution(7265506860128643885)
XLA Ops:
  7.2 0.7 copy.13
  7.9 15.7 %all_gather.10 = bf16[8,32,128]{2,0,1:T(8,128)(2,1)S(1)} all-gather(bf16[8,4,128]{2,0,1:T(8,128)(2,1)S(1)} %copy.13), channel_id=1, replica_groups=mesh['blk'=4,'grp'=8] {'grp'}, dimensions={1}, use_global_device_ids=true | all-gather | bytes 73728 | tf_op jit(solution)/shard_map/all_gather | solution.py:53
  23.6 9.0 %all_gather.11 = bf16[32,32,128]{2,1,0:T(8,128)(2,1)S(1)} all-gather(bf16[8,32,128]{2,1,0:T(8,128)(2,1)S(1)} %copy.14), channel_id=1, replica_groups=mesh['blk'=4,'grp'=8] {'blk'}, dimensions={0}, use_global_device_ids=true | all-gather | bytes 327680 | tf_op jit(solution)/shard_map/all_gather | solution.py:70
  32.6 0.7 copy-done.5
  33.3 0.6 dynamic-slice
  34.5 0.6 copy-done.4
  35.2 0.2 dynamic-update-slice
  35.3 7.3 %all-reduce = s32[32]{0:T(128)S(1)} all-reduce(s32[32]{0:T(128)S(1)} %dynamic-update-slice), channel_id=1, replica_groups=mesh['blk'=4,'grp'=8] {'blk'}, use_global_device_ids=true, to_apply=%add | all-reduce | flops 32 | bytes 256
  42.8 0.9 copy-done
  43.6 20.4 %while.20 = (s32[]{:T(128)}, f32[1024,128]{1,0:T(8,128)S(1)}, f32[]{:T(128)}, f32[256,4,128]{2,1,0:T(4,128)S(1)}, s32[32]{0:T(128)S(1)}, /*index=5*/s32[32]{0:T(...) while((s32[]{:T(128)}, f32[1024,128]{1,0:T(8,128)S(1)}, ...), condition=%wide.region_6.7_spmd.clone, body=%wide.region_0.6_spmd.clone.sunk | while | flops 207619808 | bytes 8279771 | solution.py:92
  43.7 0.7 iota_compare_fusion.3
  44.3 0.4 fusion.31
  44.7 0.4 fusion.32
  45.0 0.4 multiply_reduce_fusion.2
  45.5 0.1 reshape.110
  45.5 0.1 dynamic_slice.51
  45.6 0.2 select_reduce_fusion.2
  45.8 0.7 fusion.33
  46.5 0.1 fusion.34
  46.7 0.1 select_n.116
  46.8 0.5 multiply_convert_fusion.2
  47.2 0.3 fusion.36
  47.6 0.5 convolution_add_fusion.2
  48.7 0.7 iota_compare_fusion.3
  49.4 0.4 fusion.31
  49.8 0.4 fusion.32
  50.1 0.4 multiply_reduce_fusion.2
  50.6 0.1 reshape.110
  50.6 0.1 dynamic_slice.51
  50.7 0.2 select_reduce_fusion.2
  50.9 0.7 fusion.33
  51.6 0.1 fusion.34
  51.8 0.1 select_n.116
  51.9 0.5 multiply_convert_fusion.2
  52.3 0.3 fusion.36
  52.7 0.5 convolution_add_fusion.2
  53.8 0.7 iota_compare_fusion.3
  54.5 0.4 fusion.31
  54.9 0.4 fusion.32
  55.2 0.4 multiply_reduce_fusion.2
  55.7 0.1 reshape.110
  55.7 0.1 dynamic_slice.51
  55.8 0.2 select_reduce_fusion.2
  56.0 0.7 fusion.33
  56.7 0.1 fusion.34
  56.9 0.1 select_n.116
  56.9 0.5 multiply_convert_fusion.2
  57.4 0.3 fusion.36
  57.8 0.5 convolution_add_fusion.2
  58.9 0.7 iota_compare_fusion.3
  59.6 0.4 fusion.31
  60.0 0.4 fusion.32
  60.3 0.4 multiply_reduce_fusion.2
  60.8 0.1 reshape.110
  60.9 0.2 select_reduce_fusion.2
  61.1 0.7 fusion.33
  61.8 0.1 fusion.34
  62.0 0.1 select_n.116
  62.0 0.5 multiply_convert_fusion.2
  62.5 0.3 fusion.36
  62.9 0.5 convolution_add_fusion.2
  64.0 0.8 copy-done.2
  64.8 129.3 %all-reduce.4.cloned.1.call-done = f32[256,4,128]{2,1,0:T(4,128)} async-done(((f32[256,4,128]{2,1,0:T(4,128)}), f32[256,4,128]{2,1,0:T(4,128)}) %all-reduce.4.cloned.1.call-update) | async-done | bytes 524304
  194.1 1.3 constant_dynamic-slice_fusion.1
  (31 shorter events, 0.7 us)
Async XLA Ops:
  7.2 187.0 %all-reduce.4.cloned.1.call-start = ((), (), s32[]{:S(2)}) async-start(), calls=%async_computation | async-start | bytes 1048576
  32.6 0.7 copy-start.5
  34.5 0.7 copy-start.4
  42.7 0.9 copy-start
  42.8 0.9 copy-start.3
  64.0 0.8 copy-start.2
  64.0 131.5 %copy-start.1 = (f32[1024,128]{1,0:T(8,128)}, f32[1024,128]{1,0:T(8,128)S(1)}, u32[]{:S(2)}) copy-start(f32[1024,128]{1,0:T(8,128)S(1)} %get-tuple-element.227) | copy-start | bytes 1572868
Sparse Core Ops, SparseCore 0:
  65.0 129.1 all-reduce.3
where the time goes:
time: 204 us; the launch traced here: 203 us
  waiting for transfers between devices  129 us (63%)
  blocking collectives  32 us (16%)
  between operations  15.9 us (8%)
  other arithmetic  11.7 us (6%)
  local copies, waits for them, and re-layouts  6.99 us (3%)
  matrix products  4.52 us (2%)
  loops' own time  2.95 us (1%)
    unnamed x2, waiting for transfers between devices  129 us
    all_gather x1, blocking collectives, local(): gathered = lax.all_gather(queries, 'grp', axis=1, tiled=True)  15.7 us
    all_gather x1, blocking collectives, local(): piece_queries = lax.all_gather(gathered, 'blk', axis=0, tiled=True)  8.99 us
    unnamed x1, blocking collectives  7.34 us
    unnamed x17, local copies, waits for them, and re-layouts  5.76 us
  transfers between devices with their start and end apart: 1, of which 1 were waited for; matrix products, arithmetic and copies ran while one was open for 0% of the time, Pallas kernels for 0%

commit v1 on v0

--- a/solution.py
+++ b/solution.py
@@ -2,10 +2,27 @@
 import jax.numpy as jnp
 from jax import lax
 from jax.sharding import PartitionSpec as P
+from jax.lax import axis_index, axis_size, ppermute
 
 align_sharpness = 4.0
 logit_scale = 2.0
 logit_bias = -5.0
+
+
+def apply_the_lines(peer_axis, vals):
+    shares = axis_size(peer_axis)
+    leaves = []
+    for it in range(1, shares):
+        leaves.append((it - 1, it))
+    x_now = vals
+    oldest = leaves + [(shares - 1, 0)]
+    pieces_in = [x_now]
+    for _ in range(shares - 1):
+        x_now = ppermute(x_now, peer_axis, perm=oldest)
+        pieces_in += [x_now]
+    r2 = jnp.concatenate([*reversed(pieces_in)], axis=1)
+    next_value = jnp.roll(r2, (axis_index(peer_axis) + 1) * x_now.shape[1], axis=1)
+    return next_value
 
 
 def align(query_rows, counts, page_rows, patch_count, label_column):
@@ -50,7 +67,7 @@
     blocks = lax.axis_size("blk")
     groups = lax.axis_size("grp")
     block_queries = token_counts.shape[0]
-    gathered = lax.all_gather(queries, "grp", axis=1, tiled=True)
+    gathered = apply_the_lines("grp", vals=queries)
     query_tokens = gathered.shape[1]
     total_queries = block_queries * blocks
     empty_page = jnp.zeros(page_rows.shape, jnp.float32)

time: 204 us -> 216 us (1.059)
  waiting for transfers between devices: 129 us -> 156 us
  blocking collectives: 32 us -> 16.8 us
    ppermute x0 -> x7, waiting for transfers between devices: none -> 29.9 us  [apply_the_lines(): x_now = ppermute(x_now, peer_axis, perm=oldest)]
    all_gather x1 -> x0, blocking collectives: 15.7 us -> none  [local(): gathered = lax.all_gather(queries, 'grp', axis=1, tiled=True)]
    unnamed x2, waiting for transfers between devices: 129 us -> 127 us
    unnamed x17 -> x18, local copies, waits for them, and re-layouts: 5.76 us -> 5.05 us
  transfers between devices with their start and end apart: 1 -> 8, of which waited for: 1 -> 7; matrix products, arithmetic and copies ran while one was open for 0% -> 0% of each run, Pallas kernels for 0% -> 0%
where the time goes in v1:
time: 216 us
  waiting for transfers between devices  156 us (72%)
  blocking collectives  16.8 us (8%)
  between operations  15.9 us (7%)
  other arithmetic  11.8 us (5%)
  local copies, waits for them, and re-layouts  6.56 us (3%)
  matrix products  4.52 us (2%)
  loops' own time  2.94 us (1%)
    unnamed x2, waiting for transfers between devices  127 us
    ppermute x7, waiting for transfers between devices, apply_the_lines(): x_now = ppermute(x_now, peer_axis, perm=oldest)  29.9 us
    all_gather x1, blocking collectives, local(): piece_queries = lax.all_gather(gathered, 'blk', axis=0, tiled=True)  8.97 us
    unnamed x1, blocking collectives  7.87 us
    unnamed x18, local copies, waits for them, and re-layouts  5.05 us
  transfers between devices with their start and end apart: 8, of which 7 were waited for; matrix products, arithmetic and copies ran while one was open for 0% of the time, Pallas kernels for 0%

profile of v1, /device:TPU:0, one launch (start us, length us, event | category | flops | bytes accessed | tf_op | source)
XLA Modules:
  0.0 215.6 jit_solution(10955283956107538234)
XLA Ops:
  7.2 0.5 collective-permute-start
  7.8 5.6 %collective-permute-done = bf16[8,4,128]{2,1,0:T(4,128)(2,1)S(1)} collective-permute-done((bf16[8,4,128]{2,1,0:T(4,128)(2,1)}, bf16[8,4,128]{2,1,0:T(4,128)(2,1)S(1)}, u32[]{:S(2)}, u32[]{:S(2)}) %collective-permute-start) | collective-permute-done | bytes 8224 | tf_op jit(solution)/shard_map/ppermute | solution.py:21
  13.3 4.9 %collective-permute-done.1 = bf16[8,4,128]{2,1,0:T(4,128)(2,1)S(1)} collective-permute-done((bf16[8,4,128]{2,1,0:T(4,128)(2,1)S(1)}, bf16[8,4,128]{2,1,0:T(4,128)(2,1)S(1)}, u32[]{:S(2)}, u32[]{:S(2)}) %collective-permute-start.1) | collective-permute-done | bytes 8224 | tf_op jit(solution)/shard_map/ppermute | solution.py:21
  18.2 4.9 %collective-permute-done.2 = bf16[8,4,128]{2,1,0:T(4,128)(2,1)S(1)} collective-permute-done((bf16[8,4,128]{2,1,0:T(4,128)(2,1)S(1)}, bf16[8,4,128]{2,1,0:T(4,128)(2,1)S(1)}, u32[]{:S(2)}, u32[]{:S(2)}) %collective-permute-start.2) | collective-permute-done | bytes 8224 | tf_op jit(solution)/shard_map/ppermute | solution.py:21
  23.1 4.9 %collective-permute-done.3 = bf16[8,4,128]{2,1,0:T(4,128)(2,1)S(1)} collective-permute-done((bf16[8,4,128]{2,1,0:T(4,128)(2,1)S(1)}, bf16[8,4,128]{2,1,0:T(4,128)(2,1)S(1)}, u32[]{:S(2)}, u32[]{:S(2)}) %collective-permute-start.3) | collective-permute-done | bytes 8224 | tf_op jit(solution)/shard_map/ppermute | solution.py:21
  28.0 4.9 %collective-permute-done.4 = bf16[8,4,128]{2,1,0:T(4,128)(2,1)S(1)} collective-permute-done((bf16[8,4,128]{2,1,0:T(4,128)(2,1)S(1)}, bf16[8,4,128]{2,1,0:T(4,128)(2,1)S(1)}, u32[]{:S(2)}, u32[]{:S(2)}) %collective-permute-start.4) | collective-permute-done | bytes 8224 | tf_op jit(solution)/shard_map/ppermute | solution.py:21
  32.8 4.9 %collective-permute-done.5 = bf16[8,4,128]{2,1,0:T(4,128)(2,1)S(1)} collective-permute-done((bf16[8,4,128]{2,1,0:T(4,128)(2,1)S(1)}, bf16[8,4,128]{2,1,0:T(4,128)(2,1)S(1)}, u32[]{:S(2)}, u32[]{:S(2)}) %collective-permute-start.5) | collective-permute-done | bytes 8224 | tf_op jit(solution)/shard_map/ppermute | solution.py:21
  37.7 0.6 copy-done.6
  38.4 0.6 dynamic-slice
  39.6 0.6 copy-done.5
  40.3 0.2 dynamic-update-slice
  40.4 7.9 %all-reduce = s32[32]{0:T(128)S(1)} all-reduce(s32[32]{0:T(128)S(1)} %dynamic-update-slice), channel_id=1, replica_groups=mesh['blk'=4,'grp'=8] {'blk'}, use_global_device_ids=true, to_apply=%add | all-reduce | flops 32 | bytes 256
  48.3 0.3 concatenate.6
  48.6 9.0 %all_gather.7 = bf16[32,32,128]{2,1,0:T(8,128)(2,1)S(1)} all-gather(bf16[8,32,128]{2,1,0:T(8,128)(2,1)S(1)} %constant_dynamic-slice_fusion.2), channel_id=1, replica_groups=mesh['blk'=4,'grp'=8] {'blk'}, dimensions={0}, use_global_device_ids=true | all-gather | bytes 327680 | tf_op jit(solution)/shard_map/all_gather | solution.py:87
  57.7 0.9 copy-done
  58.5 20.4 %while.20 = (s32[]{:T(128)}, f32[1024,128]{1,0:T(8,128)S(1)}, f32[]{:T(128)}, f32[256,4,128]{2,1,0:T(4,128)S(1)}, s32[32]{0:T(128)S(1)}, /*index=5*/s32[32]{0:T(...) while((s32[]{:T(128)}, f32[1024,128]{1,0:T(8,128)S(1)}, ...), condition=%wide.region_6.7_spmd.clone, body=%wide.region_0.6_spmd.clone.sunk | while | flops 207619808 | bytes 8279771 | solution.py:109
  58.5 0.7 iota_compare_fusion.3
  59.2 0.4 fusion.31
  59.6 0.4 fusion.32
  59.9 0.4 multiply_reduce_fusion.2
  60.4 0.1 reshape.110
  60.5 0.2 select_reduce_fusion.2
  60.7 0.7 fusion.33
  61.4 0.1 fusion.34
  61.6 0.1 select_n.131
  61.6 0.5 multiply_convert_fusion.2
  62.1 0.3 fusion.36
  62.5 0.5 convolution_add_fusion.2
  63.6 0.7 iota_compare_fusion.3
  64.3 0.4 fusion.31
  64.7 0.4 fusion.32
  65.0 0.4 multiply_reduce_fusion.2
  65.5 0.1 reshape.110
  65.6 0.2 select_reduce_fusion.2
  65.8 0.7 fusion.33
  66.5 0.1 fusion.34
  66.7 0.1 select_n.131
  66.7 0.5 multiply_convert_fusion.2
  67.2 0.3 fusion.36
  67.6 0.5 convolution_add_fusion.2
  68.7 0.7 iota_compare_fusion.3
  69.4 0.4 fusion.31
  69.8 0.4 fusion.32
  70.1 0.4 multiply_reduce_fusion.2
  70.6 0.1 reshape.110
  70.7 0.2 select_reduce_fusion.2
  70.9 0.7 fusion.33
  71.8 0.1 select_n.131
  71.8 0.5 multiply_convert_fusion.2
  72.3 0.3 fusion.36
  72.7 0.5 convolution_add_fusion.2
  73.8 0.7 iota_compare_fusion.3
  74.5 0.4 fusion.31
  74.9 0.4 fusion.32
  75.2 0.4 multiply_reduce_fusion.2
  75.8 0.2 select_reduce_fusion.2
  76.0 0.7 fusion.33
  76.9 0.1 select_n.131
  76.9 0.5 multiply_convert_fusion.2
  77.4 0.3 fusion.36
  77.8 0.5 convolution_add_fusion.2
  78.9 0.8 copy-done.2
  79.7 126.5 %all-reduce.4.cloned.1.call-done = f32[256,4,128]{2,1,0:T(4,128)} async-done(((f32[256,4,128]{2,1,0:T(4,128)}), f32[256,4,128]{2,1,0:T(4,128)}) %all-reduce.4.cloned.1.call-update) | async-done | bytes 524304
  206.3 1.3 constant_dynamic-slice_fusion.1
  (46 shorter events, 1.2 us)
Async XLA Ops:
  7.2 199.1 %all-reduce.4.cloned.1.call-start = ((), (), s32[]{:S(2)}) async-start(), calls=%async_computation | async-start | bytes 1048576
  7.2 6.1 %collective-permute-start = (bf16[8,4,128]{2,1,0:T(4,128)(2,1)}, bf16[8,4,128]{2,1,0:T(4,128)(2,1)S(1)}, u32[]{:S(2)}, u32[]{:S(2)}) collective-permute-start(bf16[8,4,128]{2,1,0:T(4,128)(2,1)} %param.7), channel_id=1, source_target_pairs={{0,1},{1,2},{2,3},{3,4},{4,5},{5,6},{6,7},{7,0},{8,9},{9,10},{10,1... | collective-permute-start | bytes 24584 | tf_op jit(solution)/shard_map/ppermute | solution.py:21
  13.3 4.9 %collective-permute-start.1 = (bf16[8,4,128]{2,1,0:T(4,128)(2,1)S(1)}, bf16[8,4,128]{2,1,0:T(4,128)(2,1)S(1)}, u32[]{:S(2)}, u32[]{:S(2)}) collective-permute-start(bf16[8,4,128]{2,1,0:T(4,128)(2,1)S(1)} %collective-permute-done), channel_id=1, source_target_pairs={{0,1},{1,2},{2,3},{3,4},{4,5},{5,6},{6,7},{7,0},{8,9},{9,10},{10,1... | collective-permute-start | bytes 24584 | tf_op jit(solution)/shard_map/ppermute | solution.py:21
  18.2 4.9 %collective-permute-start.2 = (bf16[8,4,128]{2,1,0:T(4,128)(2,1)S(1)}, bf16[8,4,128]{2,1,0:T(4,128)(2,1)S(1)}, u32[]{:S(2)}, u32[]{:S(2)}) collective-permute-start(bf16[8,4,128]{2,1,0:T(4,128)(2,1)S(1)} %collective-permute-done.1), channel_id=1, source_target_pairs={{0,1},{1,2},{2,3},{3,4},{4,5},{5,6},{6,7},{7,0},{8,9},{9,10},{10,1... | collective-permute-start | bytes 24584 | tf_op jit(solution)/shard_map/ppermute | solution.py:21
  23.1 4.9 %collective-permute-start.3 = (bf16[8,4,128]{2,1,0:T(4,128)(2,1)S(1)}, bf16[8,4,128]{2,1,0:T(4,128)(2,1)S(1)}, u32[]{:S(2)}, u32[]{:S(2)}) collective-permute-start(bf16[8,4,128]{2,1,0:T(4,128)(2,1)S(1)} %collective-permute-done.2), channel_id=1, source_target_pairs={{0,1},{1,2},{2,3},{3,4},{4,5},{5,6},{6,7},{7,0},{8,9},{9,10},{10,1... | collective-permute-start | bytes 24584 | tf_op jit(solution)/shard_map/ppermute | solution.py:21
  28.0 4.9 %collective-permute-start.4 = (bf16[8,4,128]{2,1,0:T(4,128)(2,1)S(1)}, bf16[8,4,128]{2,1,0:T(4,128)(2,1)S(1)}, u32[]{:S(2)}, u32[]{:S(2)}) collective-permute-start(bf16[8,4,128]{2,1,0:T(4,128)(2,1)S(1)} %collective-permute-done.3), channel_id=1, source_target_pairs={{0,1},{1,2},{2,3},{3,4},{4,5},{5,6},{6,7},{7,0},{8,9},{9,10},{10,1... | collective-permute-start | bytes 24584 | tf_op jit(solution)/shard_map/ppermute | solution.py:21
  32.8 4.9 %collective-permute-start.5 = (bf16[8,4,128]{2,1,0:T(4,128)(2,1)S(1)}, bf16[8,4,128]{2,1,0:T(4,128)(2,1)S(1)}, u32[]{:S(2)}, u32[]{:S(2)}) collective-permute-start(bf16[8,4,128]{2,1,0:T(4,128)(2,1)S(1)} %collective-permute-done.4), channel_id=1, source_target_pairs={{0,1},{1,2},{2,3},{3,4},{4,5},{5,6},{6,7},{7,0},{8,9},{9,10},{10,1... | collective-permute-start | bytes 24584 | tf_op jit(solution)/shard_map/ppermute | solution.py:21
  37.7 10.6 %collective-permute-start.6 = (bf16[8,4,128]{2,1,0:T(4,128)(2,1)S(1)}, bf16[8,4,128]{2,1,0:T(4,128)(2,1)S(1)}, u32[]{:S(2)}, u32[]{:S(2)}) collective-permute-start(bf16[8,4,128]{2,1,0:T(4,128)(2,1)S(1)} %collective-permute-done.5), channel_id=1, source_target_pairs={{0,1},{1,2},{2,3},{3,4},{4,5},{5,6},{6,7},{7,0},{8,9},{9,10},{10,1... | collective-permute-start | bytes 24584 | tf_op jit(solution)/shard_map/ppermute | solution.py:21
  37.7 0.7 copy-start.6
  37.7 10.6 %copy-start.4 = (bf16[8,4,128]{2,1,0:T(4,128)(2,1)S(1)}, bf16[8,4,128]{2,1,0:T(4,128)(2,1)}, u32[]{:S(2)}) copy-start(bf16[8,4,128]{2,1,0:T(4,128)(2,1)} %param.7) | copy-start | bytes 24580
  39.6 0.7 copy-start.5
  57.6 1.0 copy-start
  57.7 0.9 copy-start.3
  78.9 0.8 copy-start.2
  78.9 128.7 %copy-start.1 = (f32[1024,128]{1,0:T(8,128)}, f32[1024,128]{1,0:T(8,128)S(1)}, u32[]{:S(2)}) copy-start(f32[1024,128]{1,0:T(8,128)S(1)} %get-tuple-element.227) | copy-start | bytes 1572868
Sparse Core Ops, SparseCore 0:
  79.9 126.3 all-reduce.3
